TPU v7x, 32 devices: a whole 2x2x4 slice. The times are simulated.
32 devices in a mesh: seq: 8 (over z, y), head: 4 (over x, core).
Axes of the slice: x: 2, y: 2, z: 4, core: 2. Of those that a mesh axis runs over, the one named last changes fastest.
Arguments:
- image_patches: bfloat16 [8, 256, 1152], P('seq', None, 'head'), may hold values from -6 to 6
- text_embed: bfloat16 [2048, 2048], P('seq', 'head'), may hold values from -6 to 6
- image_start: int32 [8], replicated, may hold values from 0 to 30, as said below
- image_forget: float32 [8], replicated, may hold values from 0.001 to 0.3
- adapter: bfloat16 [1152, 2048], P('head'), may hold values from -0.1875 to 0.1875
- norm_gain: float32 [2048], replicated, may hold values from 0.5 to 1.5
- in_proj: bfloat16 [2048, 4, 2048], P(None, None, 'head'), may hold values from -0.125 to 0.125
- decay_proj: bfloat16 [2048, 16], P(None, 'head'), may hold values from -0.125 to 0.125
- head_decay_ceiling: float32 [16], P('head'), may hold values from 0 to 1, as said below
- out_gain: float32 [16, 128], P('head'), may hold values from 0.5 to 1.5
- out_proj: bfloat16 [2048, 2048], P('head'), may hold values from -0.125 to 0.125
Outputs:
- image_out: bfloat16 [8, 256, 2048], P('seq', None, 'head')
- text_out: bfloat16 [2048, 2048], P('seq', 'head')
Inputs may be any that keep to these rules, and one draw needn't show every extreme that they name: `image_start`: each entry is even; the images take distinct pairs of blocks. The merged piece of 512 tokens on one device of seq never holds both the image and the text that one device of seq holds in the source layout. `head_decay_ceiling`: Positive.
All inputs are finite; a program needn't handle non-finite values.
Results may differ from a plain program's by a relative error of at most 0.0095.
Values may be sent and summed in bfloat16 or wider, within the bound.
A program may use at most 128 MiB of HBM per device.

v0:
```python
import jax
import jax.numpy as jnp
from jax import lax
from jax.sharding import PartitionSpec as P

EPSILON = 1e-06


def prefix(array, axis, join, neutral):
    place = lax.axis_index(axis)
    gathered = jax.tree.map(
        lambda a, kind: lax.all_gather(a.astype(kind), axis), array, (jnp.bfloat16, jnp.bfloat16)
    )
    state = jax.tree.map(lambda a, e: jnp.zeros_like(a) + jnp.asarray(e, a.dtype), array, neutral)

    def one(step, state):
        return join(
            state,
            jax.tree.map(
                lambda a, own: lax.dynamic_index_in_dim(a, step, 0, False).astype(own.dtype),
                gathered,
                array,
            ),
        )

    return lax.fori_loop(0, place, one, state)


def rms_scale(values, gain_row):
    mean_square = jnp.mean(values * values, axis=-1, keepdims=True)
    return values * lax.rsqrt(mean_square + EPSILON) * gain_row


def shards(
    image_patches,
    text_embed,
    image_start,
    image_forget,
    adapter,
    norm_gain,
    in_proj,
    decay_proj,
    head_decay_ceiling,
    out_gain,
    out_proj,
):
    seq_count = lax.axis_size("seq")
    my_index = lax.axis_index("seq")
    patch_row_block = text_embed.shape[0]
    local_width = text_embed.shape[1]
    share_rows = patch_row_block // seq_count
    unit_count = 2 * seq_count
    token_rows = 2 * patch_row_block
    unit_ids = jnp.arange(unit_count, dtype=jnp.int32)
    device_ids = jnp.arange(seq_count, dtype=jnp.int32)
    unit_of_image = image_start // 2
    image_hits = (unit_of_image[:, None] == unit_ids[None, :]).astype(jnp.int32)
    is_image = jnp.sum(image_hits, axis=0)
    image_here = jnp.sum(image_hits * device_ids[:, None], axis=0)
    is_text = 1 - is_image
    text_here = jnp.cumsum(is_text) - is_text
    text_pick = ((is_text[None, :] == 1) & (text_here[None, :] == device_ids[:, None])).astype(
        jnp.int32
    )
    text_unit = jnp.sum(text_pick * unit_ids[None, :], axis=1)
    source = jnp.where(is_image == 1, image_here, text_here)
    my_units = 2 * my_index + jnp.arange(2, dtype=jnp.int32)
    unit_image = jnp.take(is_image, my_units)
    partial_value = jnp.dot(image_patches[0], adapter, preferred_element_type=jnp.float32)
    embedded = lax.psum_scatter(partial_value, "head", scatter_dimension=1, tiled=True).astype(
        jnp.bfloat16
    )
    units_here = jnp.stack([embedded, text_embed]).reshape(2, seq_count, share_rows, local_width)
    spread = lax.all_to_all(units_here, "seq", split_axis=1, concat_axis=1, tiled=True)
    table = spread.reshape(unit_count, share_rows, local_width)
    pick_index = is_text * seq_count + source
    outgoing_units = jnp.take(table, pick_index, axis=0).reshape(
        seq_count, 2, share_rows, local_width
    )
    arrived = lax.all_to_all(outgoing_units, "seq", split_axis=0, concat_axis=2, tiled=True)
    merged = arrived.reshape(token_rows, local_width)
    full_rows = lax.all_gather(merged, "head", axis=1, tiled=True)
    normed = rms_scale(full_rows.astype(jnp.float32), norm_gain).astype(jnp.bfloat16)
    model_width = in_proj.shape[0]
    head_count = head_decay_ceiling.shape[0]
    head_width = out_gain.shape[1]
    projected = jnp.dot(
        normed, in_proj.reshape(model_width, -1), preferred_element_type=jnp.float32
    )
    projected = projected.astype(jnp.bfloat16).reshape(token_rows, 4, head_count, head_width)
    gate_preactivation = jnp.dot(normed, decay_proj, preferred_element_type=jnp.float32)
    forget_element = jnp.where(
        unit_image == 1, jnp.log1p(-jnp.take(image_forget, jnp.take(image_here, my_units))), 0.0
    )
    start_offsets = jnp.arange(token_rows, dtype=jnp.int32) % patch_row_block == 0
    surge_logarithm = jnp.where(start_offsets, jnp.repeat(forget_element, patch_row_block), 0.0)
    decay_logarithm = (
        -head_decay_ceiling[None, :] * jax.nn.sigmoid(gate_preactivation) + surge_logarithm[:, None]
    )
    queries = projected[:, 0]
    key_rows = projected[:, 1]
    value_rows = projected[:, 2]
    gate_rows = projected[:, 3]
    within = jnp.cumsum(decay_logarithm, axis=0)
    span_decay = within[-1]
    scores = jnp.einsum("thd,shd->hts", queries, key_rows, preferred_element_type=jnp.float32)
    lagged = within.T[:, :, None] - within.T[:, None, :]
    row_ids = jnp.arange(token_rows, dtype=jnp.int32)
    causal = (row_ids[:, None] >= row_ids[None, :])[None]
    weights = jnp.where(causal, scores * jnp.exp(jnp.where(causal, lagged, 0.0)), 0.0).astype(
        jnp.bfloat16
    )
    inner_part = jnp.einsum("hts,shd->thd", weights, value_rows, preferred_element_type=jnp.float32)
    weighted_keys = key_rows.astype(jnp.float32) * jnp.exp(span_decay[None, :] - within)[:, :, None]
    local_state = jnp.einsum(
        "thd,the->hde",
        weighted_keys,
        value_rows.astype(jnp.float32),
        precision=lax.Precision.HIGHEST,
    )

    def combine(earlier, later_part):
        return (
            earlier[0] + later_part[0],
            jnp.exp(later_part[0])[:, None, None] * earlier[1] + later_part[1],
        )

    identity = (jnp.zeros_like(span_decay), jnp.zeros_like(local_state))
    decay_before, entering = prefix((span_decay, local_state), "seq", combine, identity)
    carried = jnp.exp(within)[:, :, None] * jnp.einsum(
        "thd,hde->the", queries.astype(jnp.float32), entering, precision=lax.Precision.HIGHEST
    )
    attended = inner_part + carried
    gated = rms_scale(attended, out_gain) * jax.nn.silu(gate_rows.astype(jnp.float32))
    gated = gated.astype(jnp.bfloat16).reshape(token_rows, -1)
    partial_out = jnp.dot(gated, out_proj, preferred_element_type=jnp.float32)
    summed = lax.psum_scatter(
        partial_out.astype(jnp.bfloat16), "head", scatter_dimension=1, tiled=True
    ).astype(jnp.float32)
    result = (merged.astype(jnp.float32) + summed).astype(jnp.bfloat16)
    result_shares = result.reshape(2, seq_count, share_rows, local_width)
    back_spread = lax.all_to_all(result_shares, "seq", split_axis=1, concat_axis=1, tiled=True)
    back_table = back_spread.reshape(unit_count, share_rows, local_width)
    wanted = jnp.stack([unit_of_image, text_unit], axis=1).reshape(-1)
    back_index = wanted % 2 * seq_count + wanted // 2
    outgoing = jnp.take(back_table, back_index, axis=0).reshape(
        seq_count, 2, share_rows, local_width
    )
    returned = lax.all_to_all(outgoing, "seq", split_axis=0, concat_axis=2, tiled=True)
    image_out = returned[:, 0]
    text_out = returned[0, 1]
    return (image_out, text_out)


def solution(mesh):
    in_specs = (
        P("seq", None, "head"),
        P("seq", "head"),
        P(),
        P(),
        P("head", None),
        P(),
        P(None, None, "head"),
        P(None, "head"),
        P("head"),
        P("head", None),
        P("head", None),
    )
    out_specs = (P("seq", None, "head"), P("seq", "head"))
    return jax.shard_map(shards, mesh=mesh, in_specs=in_specs, out_specs=out_specs, check_vma=False)
```

profile of v0, /device:TPU:0, one launch (start us, length us, event | category | flops | bytes accessed | tf_op | source)
XLA Modules:
  0.0 266.6 jit_solution(11392097754306038656)
XLA Ops:
  7.2 3.6 %fusion.25 = f32[256,2048]{1,0:T(8,128)} fusion(bf16[288,2048]{1,0:T(8,128)(2,1)} %param.21, bf16[1,256,288]{1,2,0:T(8,128)(2,1)} %param.17), kind=kOutput, calls=%fused_computation.50 | convolution fusion | flops 301989888 | bytes 3424256 | tf_op jit(solution)/shard_map/dot_general | solution.py:69
  10.8 34.0 %reduce-scatter.3.cloned.1.call-done = f32[256,512]{1,0:T(8,128)} async-done(((f32[256,2048]{1,0:T(8,128)}), f32[256,512]{1,0:T(8,128)}) %reduce-scatter.3.cloned.1.call-update) | async-done | bytes 524304 | tf_op jit(solution)/shard_map/reduce_scatter | solution.py:70
  44.9 1.1 convert_element_type.68
  46.0 0.8 pad_maximum_fusion
  46.8 5.6 %all-to-all-start = ((bf16[2,8,32,512]{3,2,0,1:T(8,128)(2,1)}), bf16[2,8,32,512]{3,2,0,1:T(8,128)(2,1)S(1)}, u32[]{:S(2)}, u32[]{:S(2)}) async-start(bf16[2,8,32,512]{3,2,0,1:T(8,128)(2,1)} %pad_maximum_fusion), calls=%async_computation.1 | async-start | bytes 1048576 | tf_op jit(solution)/shard_map/all_to_all | solution.py:74
  52.8 0.1 reduce
  52.9 13.9 %all-to-all-done = bf16[2,8,32,512]{3,2,0,1:T(8,128)(2,1)S(1)} async-done(((bf16[2,8,32,512]{3,2,0,1:T(8,128)(2,1)}), bf16[2,8,32,512]{3,2,0,1:T(8,128)(2,1)S(1)}, u32[]{:S(2)}, u32[]{:S(2)}) %all-to-all-start) | async-done | bytes 524320 | tf_op jit(solution)/shard_map/all_to_all | solution.py:74
  66.8 0.6 gather_fusion.1
  67.4 0.1 broadcast_select_fusion.1
  67.6 18.0 %all_to_all.43 = bf16[8,2,32,512]{3,2,1,0:T(8,128)(2,1)S(1)} all-to-all(bf16[8,2,32,512]{3,2,1,0:T(8,128)(2,1)S(1)} %bitcast.109), channel_id=1, replica_groups=mesh['seq'=8,'head'=4] {'seq'}, dimensions={0} | all-to-all | bytes 1048576 | tf_op jit(solution)/shard_map/all_to_all | solution.py:80
  85.6 0.9 copy.135
  86.6 0.6 gather_fusion.3
  87.2 0.6 gather_fusion.2
  87.9 0.6 gather_fusion
  88.6 10.6 %copy.155 = bf16[256,8,4,512]{3,1,2,0:T(8,128)(2,1)} copy(bf16[256,8,4,512]{3,2,1,0:T(4,128)(2,1)} %bitcast.103) | data formatting | bytes 16777216
  99.2 8.1 %all-gather.5.cloned.1.call-done = bf16[512,2048]{1,0:T(8,128)(2,1)} async-done(((bf16[512,512]{1,0:T(8,128)(2,1)}), bf16[512,2048]{1,0:T(8,128)(2,1)}) %all-gather.5.cloned.1.call-update) | async-done | bytes 2097168 | tf_op jit(solution)/shard_map/all_gather | solution.py:82
  107.3 2.1 fusion
  109.4 2.3 fusion.12
  111.8 1.2 reduce-window.18
  113.0 0.2 slice_reduce_fusion
  113.1 0.2 reduce-window.19
  113.4 0.2 slice_reduce_fusion.1
  113.7 9.9 %convolution_convert_fusion.1 = bf16[512,2048]{1,0:T(8,128)(2,1)} fusion(bf16[2048,2048]{1,0:T(8,128)(2,1)} %bitcast.104, bf16[512,2048]{1,0:T(8,128)(2,1)} %all-gather.5.cloned.1.call-done, f32[2048]{0:T(1024)S(1)} %copy-done.7, f32[512]{0:T(512)S(1)} %add_rsqrt_fusion.1), kind=kOutput, calls=%fused_computation.14 | convolution fusion | flops 4300210176 | bytes 12593152 | tf_op jit(solution)/shard_map/dot_general | solution.py:87
  123.5 4.4 %reshape.189 = bf16[512,4,4,128]{3,2,1,0:T(4,128)(2,1)} reshape(bf16[512,2048]{1,0:T(8,128)(2,1)} %convolution_convert_fusion.1) | data formatting | bytes 4194304 | tf_op jit(solution)/shard_map/reshape | solution.py:90
  128.0 3.2 %fusion.41 = (bf16[512,1,4,128]{3,2,1,0:T(4,128)(2,1)S(1)}, bf16[512,1,4,128]{3,2,1,0:T(4,128)(2,1)}, bf16[512,1,4,128]{3,2,1,0:T(4,128)(2,1)S(1)}, bf16[512,1,4,128]{3,2,1,0:T(4,128)(2,1)}) fusion(bf16[512,4,4,128]{3,2,1,0:T(4,128)(2,1)} %reshape.189), kind=kLoop, calls=%fused_computation.109 | loop fusion | bytes 4194304 | tf_op jit(solution)/shard_map/slice | solution.py:103
  131.2 1.1 copy.151
  132.3 3.2 %convolution_convert_fusion.2 = bf16[4,128,128]{2,1,0:T(8,128)(2,1)} fusion(bf16[512,1,4,128]{0,3,2,1:T(8,128)(2,1)} %copy.151, f32[512,4]{0,1:T(4,128)S(1)} %get-tuple-element.112, bf16[512,1,4,128]{3,2,1,0:T(4,128)(2,1)} %get-tuple-element.108), kind=kOutput, calls=%fused_computation.22 | convolution fusion | flops 403243008 | bytes 1187840 | tf_op jit(solution)/shard_map/thd,the->hde/dot_general | solution.py:115
  135.6 0.8 iota_compare_fusion
  136.4 0.2 fusion.33
  136.5 20.7 %all-gather.1 = bf16[8,1,4]{2,1,0:T(2,128)(2,1)S(1)} all-gather(bf16[1,1,4]{2,1,0:T(2,128)(2,1)S(1)} %bitcast.124), channel_id=1, replica_groups=mesh['seq'=8,'head'=4] {'seq'}, dimensions={0}, use_global_device_ids=true | all-gather | bytes 72 | tf_op jit(solution)/shard_map/all_gather | solution.py:12
  157.2 0.1 copy.139
  157.3 0.1 copy.142
  157.4 0.3 copy.154
  157.7 4.4 %fusion.4 = f32[512,4,128]{0,2,1:T(8,128)} fusion(f32[4,512]{1,0:T(4,128)S(1)} %bitcast.120, pred[512,512]{1,0:T(8,128)(4,1)} %iota_compare_fusion, bf16[512,1,4,128]{0,3,2,1:T(8,128)(2,1)} %copy.151, bf16[512,1,4,128]{3,2,1,0:T(4,128)(2,1)} %get-tuple-element.106, bf16[512,1,4,128]{3,2,1,0:T(4,128)(2,1)} %get-tuple-element.108), kind=kOutput, calls=%fused_computation.16 | convolution fusion | flops 542113792 | bytes 2891776 | tf_op jit(solution)/shard_map/hts,shd->thd/dot_general | solution.py:113
  162.1 13.9 %all-gather.7.cloned.1.call-done = bf16[32,128,128]{2,1,0:T(8,128)(2,1)} async-done(((bf16[4,128,128]{2,1,0:T(8,128)(2,1)}), bf16[32,128,128]{2,1,0:T(8,128)(2,1)}) %all-gather.7.cloned.1.call-update) | async-done | bytes 1048592 | tf_op jit(solution)/shard_map/all_gather | solution.py:12
  176.1 2.0 multiply_reduce_fusion
  178.0 0.4 fusion.19
  178.4 2.6 convolution_convert_fusion
  181.1 37.5 %reduce-scatter.5.cloned.1.call-done = bf16[512,512]{1,0:T(8,128)(2,1)} async-done(((bf16[512,2048]{1,0:T(8,128)(2,1)}), bf16[512,512]{1,0:T(8,128)(2,1)}) %reduce-scatter.5.cloned.1.call-update) | async-done | bytes 524304 | tf_op jit(solution)/shard_map/reduce_scatter | solution.py:137
  218.6 1.2 add_convert_fusion
  219.8 0.8 copy.145
  220.6 5.5 %all-to-all-start.2 = ((bf16[2,8,32,512]{3,2,0,1:T(8,128)(2,1)}), bf16[2,8,32,512]{3,2,0,1:T(8,128)(2,1)S(1)}, u32[]{:S(2)}, u32[]{:S(2)}) async-start(bf16[2,8,32,512]{3,2,0,1:T(8,128)(2,1)} %copy.145), calls=%async_computation.4 | async-start | bytes 1048576 | tf_op jit(solution)/shard_map/all_to_all | solution.py:142
  226.1 0.1 select_reduce_fusion
  226.5 14.0 %all-to-all-done.2 = bf16[2,8,32,512]{3,2,0,1:T(8,128)(2,1)S(1)} async-done(((bf16[2,8,32,512]{3,2,0,1:T(8,128)(2,1)}), bf16[2,8,32,512]{3,2,0,1:T(8,128)(2,1)S(1)}, u32[]{:S(2)}, u32[]{:S(2)}) %all-to-all-start.2) | async-done | bytes 524320 | tf_op jit(solution)/shard_map/all_to_all | solution.py:142
  240.5 0.6 gather_fusion.4
  241.1 0.1 broadcast_select_fusion
  241.2 18.0 %all_to_all.44 = bf16[8,2,32,512]{3,2,1,0:T(8,128)(2,1)S(1)} all-to-all(bf16[8,2,32,512]{3,2,1,0:T(8,128)(2,1)S(1)} %bitcast.111), channel_id=1, replica_groups=mesh['seq'=8,'head'=4] {'seq'}, dimensions={0} | all-to-all | bytes 1048576 | tf_op jit(solution)/shard_map/all_to_all | solution.py:149
  259.3 0.8 slice_bitcast_fusion
  (62 shorter events, 1.2 us)
Async XLA Ops:
  7.2 171.3 %copy-start = (bf16[512,2048]{1,0:T(8,128)(2,1)S(1)}, bf16[512,2048]{1,0:T(8,128)(2,1)}, u32[]{:S(2)}) copy-start(bf16[512,2048]{1,0:T(8,128)(2,1)} %param.27) | copy-start | bytes 6291460
  7.2 38.8 %copy-start.4 = (bf16[256,512]{1,0:T(8,128)(2,1)S(1)}, bf16[256,512]{1,0:T(8,128)(2,1)}, u32[]{:S(2)}) copy-start(bf16[256,512]{1,0:T(8,128)(2,1)} %param.18) | copy-start | bytes 786436
  7.2 45.3 %copy-start.9 = (s32[8]{0:T(128)S(1)}, s32[8]{0:T(128)}, u32[]{:S(2)}) copy-start(s32[8]{0:T(128)} %param.19) | copy-start | bytes 100
  7.2 37.7 %reduce-scatter.3.cloned.1.call-start = ((), (), s32[]{:S(2)}) async-start(), calls=%async_computation.6 | async-start | bytes 2621440 | tf_op jit(solution)/shard_map/reduce_scatter | solution.py:70
  46.8 41.0 %copy-start.1 = (f32[8]{0:T(128)S(1)}, f32[8]{0:T(128)}, u32[]{:S(2)}) copy-start(f32[8]{0:T(128)} %param.20) | copy-start | bytes 100
  46.8 41.8 %copy-start.8 = (f32[4]{0:T(128)S(1)}, f32[4]{0:T(128)}, u32[]{:S(2)}) copy-start(f32[4]{0:T(128)} %param.25) | copy-start | bytes 52
  46.8 20.0 %all-to-all-start = ((bf16[2,8,32,512]{3,2,0,1:T(8,128)(2,1)}), bf16[2,8,32,512]{3,2,0,1:T(8,128)(2,1)S(1)}, u32[]{:S(2)}, u32[]{:S(2)}) async-start(bf16[2,8,32,512]{3,2,0,1:T(8,128)(2,1)} %pad_maximum_fusion), calls=%async_computation.1 | async-start | bytes 1048576 | tf_op jit(solution)/shard_map/all_to_all | solution.py:74
  52.5 54.8 %all-gather.5.cloned.1.call-start = ((), (), s32[]{:S(2)}) async-start(), calls=%async_computation.7 | async-start | bytes 2621440 | tf_op jit(solution)/shard_map/all_gather | solution.py:82
  86.5 89.5 %all-gather.7.cloned.1.call-start = ((), (), s32[]{:S(2)}) async-start(), calls=%async_computation.9 | async-start | bytes 1179648 | tf_op jit(solution)/shard_map/all_gather | solution.py:12
  88.6 20.8 %copy-start.6 = (bf16[2048,4]{0,1:T(4,128)(2,1)S(1)}, bf16[2048,4]{0,1:T(4,128)(2,1)}, u32[]{:S(2)}) copy-start(bf16[2048,4]{0,1:T(4,128)(2,1)} %param.24) | copy-start | bytes 49156
  88.6 20.8 %copy-start.7 = (f32[2048]{0:T(1024)S(1)}, f32[2048]{0:T(1024)}, u32[]{:S(2)}) copy-start(f32[2048]{0:T(1024)} %param.22) | copy-start | bytes 24580
  135.5 83.1 %reduce-scatter.5.cloned.1.call-start = ((), (), s32[]{:S(2)}) async-start(), calls=%async_computation.8 | async-start | bytes 2621440 | tf_op jit(solution)/shard_map/reduce_scatter | solution.py:137
  157.7 18.3 %copy-start.3 = (bf16[512,1,4,128]{3,2,1,0:T(4,128)(2,1)S(1)}, bf16[512,1,4,128]{3,2,1,0:T(4,128)(2,1)}, u32[]{:S(2)}) copy-start(bf16[512,1,4,128]{3,2,1,0:T(4,128)(2,1)} %get-tuple-element.106) | copy-start | bytes 1572868
  162.1 15.9 %copy-start.5 = (f32[4,128]{1,0:T(4,128)S(1)}, f32[4,128]{1,0:T(4,128)}, u32[]{:S(2)}) copy-start(f32[4,128]{1,0:T(4,128)} %param.26) | copy-start | bytes 6148
  178.4 40.2 %copy-start.2 = (bf16[1,2,8,32,512]{4,3,2,1,0:T(8,128)(2,1)S(1)}, bf16[1,2,8,32,512]{4,3,2,1,0:T(8,128)(2,1)}, u32[]{:S(2)}) copy-start(bf16[1,2,8,32,512]{4,3,2,1,0:T(8,128)(2,1)} %copy.135) | copy-start | bytes 1572868
  220.6 19.8 %all-to-all-start.2 = ((bf16[2,8,32,512]{3,2,0,1:T(8,128)(2,1)}), bf16[2,8,32,512]{3,2,0,1:T(8,128)(2,1)S(1)}, u32[]{:S(2)}, u32[]{:S(2)}) async-start(bf16[2,8,32,512]{3,2,0,1:T(8,128)(2,1)} %copy.145), calls=%async_computation.4 | async-start | bytes 1048576 | tf_op jit(solution)/shard_map/all_to_all | solution.py:142
Sparse Core Ops, SparseCore 0:
  11.0 33.8 reduce-scatter.2
  86.6 20.6 all-gather.4
  135.6 40.3 all-gather.6
  181.2 37.2 reduce-scatter.4
where the time goes:
time: 267 us
  waiting for transfers between devices  121 us (45%)
  blocking collectives  56.7 us (21%)
  matrix products  27.9 us (10%)
  local copies, waits for them, and re-layouts  26.5 us (10%)
  between operations  14.1 us (5%)
  starting transfers between devices  11.3 us (4%)
  other arithmetic  8.62 us (3%)
    reduce_scatter x1, waiting for transfers between devices, shards(): lax.psum_scatter(partial_out.astype(jnp.bfloat16), 'head', scatter_dimens...  37.5 us
    reduce_scatter x1, waiting for transfers between devices, shards(): lax.psum_scatter(partial_value, 'head', scatter_dimension=1, tiled=True)  34 us
    all_gather x1, blocking collectives, prefix(): lax.all_gather(a.astype(kind), axis)  20.7 us
    all_to_all x1, blocking collectives, shards(): lax.all_to_all(outgoing_units, 'seq', split_axis=0, concat_axis=2, tiled=...  18 us
    all_to_all x1, blocking collectives, shards(): lax.all_to_all(outgoing, 'seq', split_axis=0, concat_axis=2, tiled=True)  18 us
    all_to_all x1, waiting for transfers between devices, shards(): lax.all_to_all(result_shares, 'seq', split_axis=1, concat_axis=1, tiled=T...  14 us
    all_to_all x1, waiting for transfers between devices, shards(): lax.all_to_all(units_here, 'seq', split_axis=1, concat_axis=1, tiled=True)  13.9 us
    all_gather x1, waiting for transfers between devices, prefix(): lax.all_gather(a.astype(kind), axis)  13.9 us
  transfers between devices with their start and end apart: 6, of which 6 were waited for; matrix products, arithmetic and copies ran while one was open for 7% of the time, Pallas kernels for 0%

commit v1 on v0

v1 whole, which is shorter than its diff:
```python
import jax
import jax.numpy as jnp
from jax import lax
from jax.sharding import PartitionSpec as P

EPSILON = 1e-06


def rms_scale(values, gain_row):
    mean_square = jnp.mean(values * values, axis=-1, keepdims=True)
    return values * lax.rsqrt(mean_square + EPSILON) * gain_row


def unit_places(image_start, seq_count):
    unit_ids = jnp.arange(2 * seq_count, dtype=jnp.int32)
    device_ids = jnp.arange(seq_count, dtype=jnp.int32)
    unit_of_image = image_start // 2
    is_text = 1 - jnp.sum(
        (unit_of_image[:, None] == unit_ids[None, :]).astype(jnp.int32), axis=0
    )
    before = (unit_ids[None, :] < unit_ids[:, None]).astype(jnp.int32)
    text_here = jnp.sum(before * is_text[None, :], axis=1)
    text_pick = (is_text[None, :] == 1) & (text_here[None, :] == device_ids[:, None])
    text_unit = jnp.sum(text_pick.astype(jnp.int32) * unit_ids[None, :], axis=1)
    return jnp.stack([unit_of_image, text_unit], axis=1)


def shards(
    image_patches,
    text_embed,
    image_start,
    image_forget,
    adapter,
    norm_gain,
    in_proj,
    decay_proj,
    head_decay_ceiling,
    out_gain,
    out_proj,
):
    seq_count = lax.axis_size("seq")
    me = lax.axis_index("seq")
    rows = text_embed.shape[0]
    model_width = in_proj.shape[0]
    heads = head_decay_ceiling.shape[0]
    head_width = out_gain.shape[1]
    places = unit_places(image_start, seq_count)
    partial_value = jnp.dot(image_patches[0], adapter, preferred_element_type=jnp.float32)
    embedded = lax.psum_scatter(
        partial_value.astype(jnp.bfloat16), "head", scatter_dimension=1, tiled=True
    )
    merged = jnp.concatenate([embedded, text_embed], axis=0)
    full_rows = lax.all_gather(merged, "head", axis=1, tiled=True)
    normed = rms_scale(full_rows.astype(jnp.float32), norm_gain).astype(jnp.bfloat16)
    projected = jnp.dot(
        normed, in_proj.reshape(model_width, -1), preferred_element_type=jnp.float32
    )
    projected = projected.astype(jnp.bfloat16).reshape(2, rows, 4, heads, head_width)
    preact = jnp.dot(normed, decay_proj, preferred_element_type=jnp.float32)
    burst = jnp.log1p(-lax.dynamic_index_in_dim(image_forget, me, 0, False))
    first = jnp.arange(2 * rows, dtype=jnp.int32) == 0
    decay = -head_decay_ceiling[None, :] * jax.nn.sigmoid(preact)
    decay = (decay + jnp.where(first, burst, 0.0)[:, None]).reshape(2, rows, heads)
    queries, keys, values, gates = (projected[:, :, i] for i in range(4))
    within = jnp.cumsum(decay, axis=1)
    span = within[:, -1]
    scores = jnp.einsum("uthd,ushd->uhts", queries, keys, preferred_element_type=jnp.float32)
    across = within.transpose(0, 2, 1)
    lagged = across[:, :, :, None] - across[:, :, None, :]
    row_ids = jnp.arange(rows, dtype=jnp.int32)
    causal = row_ids[:, None] >= row_ids[None, :]
    weights = jnp.where(causal, scores * jnp.exp(jnp.where(causal, lagged, 0.0)), 0.0).astype(
        jnp.bfloat16
    )
    inner = jnp.einsum("uhts,ushd->uthd", weights, values, preferred_element_type=jnp.float32)
    weighted = keys.astype(jnp.float32) * jnp.exp(span[:, None] - within)[..., None]
    state = jnp.einsum(
        "uthd,uthe->uhde",
        weighted.astype(jnp.bfloat16),
        values,
        preferred_element_type=jnp.float32,
    )
    all_state = lax.all_gather(state.astype(jnp.bfloat16), "seq")
    all_span = lax.all_gather(span, "seq")
    mine = lax.dynamic_index_in_dim(places, me, 0, False)
    flat = places.reshape(-1)
    earlier = flat[None, :] < mine[:, None]
    between = earlier[:, None, :] & (flat[None, None, :] > flat[None, :, None])
    passed = jnp.sum(
        jnp.where(between[..., None], all_span.reshape(1, 1, 2 * seq_count, heads), 0.0), axis=2
    )
    share = jnp.where(earlier[..., None], jnp.exp(passed), 0.0)
    entering = jnp.sum(
        share[..., None, None]
        * all_state.reshape(1, 2 * seq_count, heads, head_width, head_width).astype(jnp.float32),
        axis=1,
    )
    carried = jnp.exp(within)[..., None] * jnp.einsum(
        "uthd,uhde->uthe",
        queries,
        entering.astype(jnp.bfloat16),
        preferred_element_type=jnp.float32,
    )
    attended = inner + carried
    gated = rms_scale(attended, out_gain) * jax.nn.silu(gates.astype(jnp.float32))
    gated = gated.astype(jnp.bfloat16).reshape(2 * rows, -1)
    partial_out = jnp.dot(gated, out_proj, preferred_element_type=jnp.float32)
    summed = lax.psum_scatter(
        partial_out.astype(jnp.bfloat16), "head", scatter_dimension=1, tiled=True
    ).astype(jnp.float32)
    result = (merged.astype(jnp.float32) + summed).astype(jnp.bfloat16)
    return (result[:rows][None], result[rows:])


def solution(mesh):
    in_specs = (
        P("seq", None, "head"),
        P("seq", "head"),
        P(),
        P(),
        P("head", None),
        P(),
        P(None, None, "head"),
        P(None, "head"),
        P("head"),
        P("head", None),
        P("head", None),
    )
    out_specs = (P("seq", None, "head"), P("seq", "head"))
    return jax.shard_map(shards, mesh=mesh, in_specs=in_specs, out_specs=out_specs, check_vma=False)
```

time: 267 us -> 191 us (0.72)
  blocking collectives: 56.7 us -> 20.7 us
  waiting for transfers between devices: 121 us -> 94.6 us
  starting transfers between devices: 11.3 us -> 0.16 us
  matrix products: 27.9 us -> 24.1 us
    all_to_all x2 -> x0, blocking collectives: 36.1 us -> none  [the longest x1 18 us: shards(): lax.all_to_all(outgoing_units, 'seq', split_axis=0, concat_axis=2, tiled=...]
    all_to_all x2 -> x0, waiting for transfers between devices: 27.8 us -> none  [the longest x1 14 us: shards(): lax.all_to_all(result_shares, 'seq', split_axis=1, concat_axis=1, tiled=T...]
    all_gather x1, waiting for transfers between devices: 13.9 us -> 26 us  [shards(): all_state = lax.all_gather(state.astype(jnp.bfloat16), 'seq')]
    all_to_all x2 -> x0, starting transfers between devices: 11.2 us -> none  [the longest x1 5.65 us: shards(): lax.all_to_all(units_here, 'seq', split_axis=1, concat_axis=1, tiled=True)]
    reduce_scatter x1, waiting for transfers between devices: 37.5 us -> 29.9 us  [shards(): lax.psum_scatter(partial_out.astype(jnp.bfloat16), 'head', scatter_dimens...]
    reduce_scatter x1, waiting for transfers between devices: 34 us -> 27.6 us  [shards(): lax.psum_scatter(partial_value.astype(jnp.bfloat16), 'head', scatter_dime...]
    dot_general x4, matrix products: 11.9 us -> 8.27 us  [the longest x1 3.45 us: shards(): jnp.einsum('uhts,ushd->uthd', weights, values, preferred_element_type=jnp...]
    gather x5 -> x0, local copies, waits for them, and re-layouts: 3.08 us -> none  [the longest x1 0.64 us: shards(): unit_image = jnp.take(is_image, my_units)]
  transfers between devices with their start and end apart: 6 -> 4, of which waited for: 6 -> 4; matrix products, arithmetic and copies ran while one was open for 7% -> 7% of each run, Pallas kernels for 0% -> 0%
where the time goes in v1:
time: 191 us; the launch traced here: 190 us
  waiting for transfers between devices  94.6 us (50%)
  local copies, waits for them, and re-layouts  24.9 us (13%)
  matrix products  24.1 us (13%)
  blocking collectives  20.7 us (11%)
  between operations  14.7 us (8%)
  other arithmetic  11.1 us (6%)
    reduce_scatter x1, waiting for transfers between devices, shards(): lax.psum_scatter(partial_out.astype(jnp.bfloat16), 'head', scatter_dimens...  29.9 us
    reduce_scatter x1, waiting for transfers between devices, shards(): lax.psum_scatter(partial_value.astype(jnp.bfloat16), 'head', scatter_dime...  27.6 us
    all_gather x1, waiting for transfers between devices, shards(): all_state = lax.all_gather(state.astype(jnp.bfloat16), 'seq')  26 us
    all_gather x1, blocking collectives, shards(): all_span = lax.all_gather(span, 'seq')  20.7 us
    unnamed x26, local copies, waits for them, and re-layouts  14.4 us
    all_gather x1, waiting for transfers between devices, shards(): full_rows = lax.all_gather(merged, 'head', axis=1, tiled=True)  11.1 us
    dot_general x1, matrix products, shards(): jnp.dot(normed, in_proj.reshape(model_width, -1), preferred_element_type=...  9.97 us
    reshape x1, local copies, waits for them, and re-layouts, shards(): projected.astype(jnp.bfloat16).reshape(2, rows, 4, heads, head_width)  4.44 us
  transfers between devices with their start and end apart: 4, of which 4 were waited for; matrix products, arithmetic and copies ran while one was open for 7% of the time, Pallas kernels for 0%

profile of v1, /device:TPU:0, one launch (start us, length us, event | category | flops | bytes accessed | tf_op | source)
XLA Modules:
  0.0 190.2 jit_solution(2481767828130457093)
XLA Ops:
  7.3 3.2 %convolution_convert_fusion.2 = bf16[256,2048]{1,0:T(8,128)(2,1)} fusion(bf16[288,2048]{1,0:T(8,128)(2,1)} %param.15, bf16[1,256,288]{1,2,0:T(8,128)(2,1)} %param.11), kind=kOutput, calls=%fused_computation.8 | convolution fusion | flops 302514176 | bytes 2375680 | tf_op jit(solution)/shard_map/dot_general | solution.py:48
  10.5 0.0 all-gather.5.cloned.1.call-start
  10.5 27.6 %reduce-scatter.3.cloned.1.call-done = bf16[256,512]{1,0:T(8,128)(2,1)} async-done(((bf16[256,2048]{1,0:T(8,128)(2,1)}), bf16[256,512]{1,0:T(8,128)(2,1)}) %reduce-scatter.3.cloned.1.call-update) | async-done | bytes 262160 | tf_op jit(solution)/shard_map/reduce_scatter | solution.py:49
  38.2 1.0 constant_dynamic-update-slice_fusion.1
  39.2 0.8 copy-done.1
  40.0 0.0 all-gather.7.cloned.1.call-start
  40.1 0.6 dynamic_slice.8
  41.4 10.2 %copy.109 = bf16[256,8,4,512]{3,1,2,0:T(8,128)(2,1)} copy(bf16[256,8,4,512]{3,2,1,0:T(4,128)(2,1)} %bitcast.65) | data formatting | bytes 16777216
  51.6 11.1 %all-gather.5.cloned.1.call-done = bf16[512,2048]{1,0:T(8,128)(2,1)} async-done(((bf16[512,512]{1,0:T(8,128)(2,1)}), bf16[512,2048]{1,0:T(8,128)(2,1)}) %all-gather.5.cloned.1.call-update) | async-done | bytes 2097168 | tf_op jit(solution)/shard_map/all_gather | solution.py:53
  62.7 2.2 %fusion = f32[512]{0:T(512)S(1)} fusion(bf16[512,2048]{1,0:T(8,128)(2,1)} %all-gather.5.cloned.1.call-done), kind=kLoop, calls=%fused_computation.3 | loop fusion | flops 3145216 | bytes 2099200 | tf_op jit(solution)/shard_map/reduce_sum | solution.py:10
  65.0 0.8 fusion.11
  65.8 2.4 %reduce-window.6 = f32[2,4,2,128]{3,2,1,0:T(2,128)S(1)} reduce-window(f32[2,4,2,128]{3,2,1,0:T(2,128)S(1)} %copy.104, f32[]{:T(128)} %constant.42.clone.1), window={size=1x1x1x128 pad=0_0x0_0x0_0x127_0}, to_apply=%region_2.3 | reduce-window | flops 260096 | bytes 16388 | tf_op jit(solution)/shard_map/reduce-window
  68.2 0.1 slice.39
  68.3 0.1 copy.90
  68.5 0.1 copy.91
  68.6 0.1 broadcast_add_fusion
  68.7 0.2 fusion.35
  68.8 0.1 subtract_exponential_fusion
  68.9 10.0 %convolution_convert_fusion.1 = bf16[512,2048]{1,0:T(8,128)(2,1)} fusion(bf16[2048,2048]{1,0:T(8,128)(2,1)} %bitcast.66, bf16[512,2048]{1,0:T(8,128)(2,1)} %all-gather.5.cloned.1.call-done, f32[2048]{0:T(1024)S(1)} %copy-done.7, f32[512]{0:T(512)S(1)} %add_rsqrt_fusion.1), kind=kOutput, calls=%fused_computation.7 | convolution fusion | flops 4300210176 | bytes 12593152 | tf_op jit(solution)/shard_map/dot_general | solution.py:55
  78.9 4.4 %reshape.204 = bf16[2,256,4,4,128]{4,3,2,1,0:T(4,128)(2,1)} reshape(bf16[512,2048]{1,0:T(8,128)(2,1)} %convolution_convert_fusion.1) | data formatting | bytes 4194304 | tf_op jit(solution)/shard_map/reshape | solution.py:58
  83.3 3.2 %fusion.33 = (bf16[2,256,1,4,128]{4,3,2,1,0:T(4,128)(2,1)}, bf16[2,256,1,4,128]{4,3,2,1,0:T(4,128)(2,1)S(1)}, bf16[2,256,1,4,128]{4,3,2,1,0:T(4,128)(2,1)S(1)}, bf16[2,256,1,4,128]{4,3,2,1,0:T(4,128)(2,1)}) fusion(bf16[2,256,4,4,128]{4,3,2,1,0:T(4,128)(2,1)} %reshape.204), kind=kLoop, calls=%fused_computation.78 | loop fusion | bytes 4194304 | tf_op jit(solution)/shard_map/slice | solution.py:64
  86.5 1.1 copy.105
  87.6 2.7 %convolution_convert_fusion.3 = bf16[2,4,128,128]{3,2,1,0:T(8,128)(2,1)} fusion(bf16[2,256,1,4,128]{1,4,3,0,2:T(8,128)(2,1)} %copy.105, f32[2,256,4]{1,2,0:T(4,128)S(1)} %get-tuple-element.10, bf16[2,256,1,4,128]{4,3,2,1,0:T(4,128)(2,1)} %get-tuple-element.5), kind=kOutput, calls=%fused_computation.17 | convolution fusion | flops 68026368 | bytes 1318912 | tf_op jit(solution)/shard_map/uthd,uthe->uhde/dot_general | solution.py:77
  90.4 0.1 convert_reduce_fusion
  90.5 0.1 select_reduce_fusion.1
  90.6 0.1 select_reduce_fusion.2
  90.8 0.2 dynamic-slice_reduce_fusion
  91.0 0.1 copy.92
  91.1 0.1 lt.48
  91.2 0.1 broadcast_compare_fusion.1
  91.2 0.1 broadcast_compare_fusion
  91.3 0.1 copy.93
  91.4 20.7 %all-gather = f32[16,1,4]{2,1,0:T(1,128)S(1)} all-gather(f32[2,1,4]{2,1,0:T(1,128)S(1)} %copy.93), channel_id=2, replica_groups=mesh['seq'=8,'head'=4] {'seq'}, dimensions={0}, use_global_device_ids=true | all-gather | bytes 288 | tf_op jit(solution)/shard_map/all_gather | solution.py:84
  112.1 0.1 copy.94
  112.2 0.1 select_reduce_fusion
  112.3 0.1 copy.95
  112.4 1.3 copy.108
  113.7 26.0 %all-gather.7.cloned.1.call-done = bf16[16,4,128,128]{3,2,1,0:T(8,128)(2,1)} async-done(((bf16[2,4,128,128]{3,2,1,0:T(8,128)(2,1)}), bf16[16,4,128,128]{3,2,1,0:T(8,128)(2,1)}) %all-gather.7.cloned.1.call-update) | async-done | bytes 2097168 | tf_op jit(solution)/shard_map/all_gather | solution.py:83
  139.7 2.1 %convert_element_type.85 = f32[16,4,128,128]{3,2,1,0:T(8,128)S(1)} convert(bf16[16,4,128,128]{3,2,1,0:T(8,128)(2,1)} %all-gather.7.cloned.1.call-done) | non-fusion elementwise | flops 1048576 | bytes 6291456 | tf_op jit(solution)/shard_map/convert_element_type | solution.py:95
  141.8 0.7 multiply_reduce_fusion
  142.5 1.4 fusion.6
  143.9 3.5 %multiply_reduce_fusion.1 = (f32[2,256,4]{1,2,0:T(4,128)S(1)}, f32[2,256,4,128]{1,3,2,0:T(8,128)}) fusion(f32[2,256,4,128]{1,3,2,0:T(8,128)} %fusion.6, f32[2,4,256]{2,1,0:T(4,128)S(1)} %reduce_window_sum.24, pred[256,256]{1,0:T(8,128)(4,1)S(1)} %iota_compare_fusion, bf16[2,256,1,4,128]{4,3,2,1,0:T(4,128)(2,1)S(1)} %get-tuple-element.3, ...), kind=kOutput, calls=%fused_computation.29 | convolution fusion | flops 271841280 | bytes 3751936 | tf_op jit(solution)/shard_map/uhts,ushd->uthd/dot_general | solution.py:75
  147.3 1.6 fusion.19
  148.9 0.3 copy.100
  149.2 2.6 %convolution_convert_fusion = bf16[512,2048]{1,0:T(8,128)(2,1)} fusion(bf16[512,2048]{1,0:T(8,128)(2,1)S(1)} %copy-done, bf16[64,8,4,128]{3,2,1,0:T(4,128)(2,1)S(1)} %bitcast.67), kind=kOutput, calls=%fused_computation.6 | convolution fusion | flops 1074790400 | bytes 4718592 | tf_op jit(solution)/shard_map/dot_general | solution.py:107
  151.9 29.9 %reduce-scatter.5.cloned.1.call-done = bf16[512,512]{1,0:T(8,128)(2,1)} async-done(((bf16[512,2048]{1,0:T(8,128)(2,1)}), bf16[512,512]{1,0:T(8,128)(2,1)}) %reduce-scatter.5.cloned.1.call-update) | async-done | bytes 524304 | tf_op jit(solution)/shard_map/reduce_scatter | solution.py:108
  181.7 1.2 add_convert_fusion
  182.9 0.8 fusion.34
  (46 shorter events, 0.4 us)
Async XLA Ops:
  7.2 142.0 %copy-start = (bf16[512,2048]{1,0:T(8,128)(2,1)S(1)}, bf16[512,2048]{1,0:T(8,128)(2,1)}, u32[]{:S(2)}) copy-start(bf16[512,2048]{1,0:T(8,128)(2,1)} %param.21) | copy-start | bytes 6291460
  7.2 31.9 %copy-start.4 = (bf16[256,512]{1,0:T(8,128)(2,1)S(1)}, bf16[256,512]{1,0:T(8,128)(2,1)}, u32[]{:S(2)}) copy-start(bf16[256,512]{1,0:T(8,128)(2,1)} %param.12) | copy-start | bytes 786436
  7.2 32.9 %copy-start.8 = (f32[8]{0:T(128)S(1)}, f32[8]{0:T(128)}, u32[]{:S(2)}) copy-start(f32[8]{0:T(128)} %param.14) | copy-start | bytes 100
  7.2 34.2 %copy-start.9 = (f32[4]{0:T(128)S(1)}, f32[4]{0:T(128)}, u32[]{:S(2)}) copy-start(f32[4]{0:T(128)} %param.19) | copy-start | bytes 52
  7.2 30.9 %reduce-scatter.3.cloned.1.call-start = ((), (), s32[]{:S(2)}) async-start(), calls=%async_computation.2 | async-start | bytes 1310720 | tf_op jit(solution)/shard_map/reduce_scatter | solution.py:49
  10.5 52.2 %all-gather.5.cloned.1.call-start = ((), (), s32[]{:S(2)}) async-start(), calls=%async_computation.3 | async-start | bytes 2621440 | tf_op jit(solution)/shard_map/all_gather | solution.py:53
  39.2 0.8 copy-start.1
  40.0 99.7 %all-gather.7.cloned.1.call-start = ((), (), s32[]{:S(2)}) async-start(), calls=%async_computation.5 | async-start | bytes 2359296 | tf_op jit(solution)/shard_map/all_gather | solution.py:83
  41.4 23.6 %copy-start.6 = (bf16[2048,4]{0,1:T(4,128)(2,1)S(1)}, bf16[2048,4]{0,1:T(4,128)(2,1)}, u32[]{:S(2)}) copy-start(bf16[2048,4]{0,1:T(4,128)(2,1)} %param.18) | copy-start | bytes 49156
  51.6 13.4 %copy-start.7 = (f32[2048]{0:T(1024)S(1)}, f32[2048]{0:T(1024)}, u32[]{:S(2)}) copy-start(f32[2048]{0:T(1024)} %param.16) | copy-start | bytes 24580
  62.7 2.3 %copy-start.3 = (bf16[512,2048]{1,0:T(8,128)(2,1)S(1)}, bf16[512,2048]{1,0:T(8,128)(2,1)}, u32[]{:S(2)}) copy-start(bf16[512,2048]{1,0:T(8,128)(2,1)} %all-gather.5.cloned.1.call-done) | copy-start | bytes 6291460
  86.5 3.9 %copy-start.10 = (s32[8]{0:T(128)S(1)}, s32[8]{0:T(128)}, u32[]{:S(2)}) copy-start(s32[8]{0:T(128)} %param.13) | copy-start | bytes 100
  90.3 91.4 %reduce-scatter.5.cloned.1.call-start = ((), (), s32[]{:S(2)}) async-start(), calls=%async_computation.4 | async-start | bytes 2621440 | tf_op jit(solution)/shard_map/reduce_scatter | solution.py:108
  143.9 3.5 %copy-start.5 = (f32[4,128]{1,0:T(4,128)S(1)}, f32[4,128]{1,0:T(4,128)}, u32[]{:S(2)}) copy-start(f32[4,128]{1,0:T(4,128)} %param.20) | copy-start | bytes 6148
  151.8 29.9 %copy-start.2 = (bf16[512,512]{1,0:T(8,128)(2,1)S(1)}, bf16[512,512]{1,0:T(8,128)(2,1)}, u32[]{:S(2)}) copy-start(bf16[512,512]{1,0:T(8,128)(2,1)} %copy-done.1) | copy-start | bytes 1572868
Sparse Core Ops, SparseCore 0:
  10.6 27.4 reduce-scatter.2
  40.1 22.5 all-gather.4
  90.5 49.1 all-gather.6
  152.0 29.6 reduce-scatter.4

commit v2 on v1

v2 whole, which is shorter than its diff:
```python
import functools

import jax
import jax.numpy as jnp
from jax import lax
from jax.experimental import pallas as pl
from jax.experimental.pallas import tpu as pltpu
from jax.sharding import PartitionSpec as P

EPSILON = 1e-06
LANES = 128
SPAN_ROWS = 8
BF16 = jnp.bfloat16
F32 = jnp.float32


def unit_places(image_start, seq_count):
    unit_ids = jnp.arange(2 * seq_count, dtype=jnp.int32)
    device_ids = jnp.arange(seq_count, dtype=jnp.int32)
    unit_of_image = image_start // 2
    is_text = 1 - jnp.sum(
        (unit_of_image[:, None] == unit_ids[None, :]).astype(jnp.int32), axis=0
    )
    before = (unit_ids[None, :] < unit_ids[:, None]).astype(jnp.int32)
    text_here = jnp.sum(before * is_text[None, :], axis=1)
    text_pick = (is_text[None, :] == 1) & (text_here[None, :] == device_ids[:, None])
    text_unit = jnp.sum(text_pick.astype(jnp.int32) * unit_ids[None, :], axis=1)
    return jnp.stack([unit_of_image, text_unit], axis=1)


def dot(a, b):
    return jnp.dot(a, b, preferred_element_type=F32)


def exact_dot(a, b):
    return jnp.dot(a, b, preferred_element_type=F32, precision=lax.Precision.HIGHEST)


def iota(shape, dim):
    return lax.broadcasted_iota(jnp.int32, shape, dim)


def layer_kernel(
    n,
    heads,
    patches_ref,
    text_ref,
    adapter_ref,
    gain_ref,
    decay_ref,
    ceiling_ref,
    burst_ref,
    out_gain_ref,
    place_row_ref,
    place_col_ref,
    in_proj_ref,
    out_proj_ref,
    image_out_ref,
    text_out_ref,
    w_in,
    w_out,
    gath,
    normed,
    proj,
    inner,
    within_keep,
    half_send,
    half_recv,
    own,
    cross_send,
    cross_recv,
    out_send,
    out_recv,
    out_cross_send,
    out_cross_recv,
    out_own,
    state,
    state_recv,
    entering_send,
    entering,
    span_send,
    span_recv,
    load_sem,
    pair_send_sem,
    pair_recv_sem,
    state_send_sem,
    state_recv_sem,
    span_send_sem,
    span_recv_sem,
    enter_send_sem,
    enter_recv_sem,
    keep_sem,
):
    me = lax.axis_index("seq")
    h = lax.axis_index("head")
    h1 = h + 1 - 2 * lax.rem(h, 2)
    h2 = lax.rem(h + 2, 4)
    h3 = lax.rem(h1 + 2, 4)
    rows, width = text_ref.shape
    part = heads * LANES // n
    in_load = pltpu.make_async_copy(in_proj_ref, w_in, load_sem.at[0])
    out_load = pltpu.make_async_copy(out_proj_ref, w_out, load_sem.at[1])
    in_load.start()
    out_load.start()

    barrier = pltpu.get_barrier_semaphore()
    pl.semaphore_signal(barrier, inc=1, device_id={"head": h1})
    pl.semaphore_signal(barrier, inc=1, device_id={"head": h2})
    for j in range(1, n):
        pl.semaphore_signal(barrier, inc=1, device_id={"seq": lax.rem(me + j, n)})
    pl.semaphore_wait(barrier, n + 1)

    sent = []

    def send(src, dst, index, to):
        copy = pltpu.make_async_remote_copy(
            src_ref=src,
            dst_ref=dst,
            send_sem=pair_send_sem.at[index],
            recv_sem=pair_recv_sem.at[index],
            device_id={"head": to},
        )
        copy.start()
        sent.append(copy)
        return copy

    def columns(block):
        return pl.ds(pl.multiple_of(block * width, width), width)

    text_cross = send(text_ref, gath.at[1, h], 0, h2)
    text_pair = send(text_ref, gath.at[1, h], 1, h1)
    gath[1, h] = text_ref[...]

    half_send[0] = dot(patches_ref[...], adapter_ref[:, columns(h1)]).astype(BF16)
    half_send[1] = dot(patches_ref[...], adapter_ref[:, columns(h3)]).astype(BF16)
    half = send(half_send, half_recv, 2, h1)
    far = dot(patches_ref[...], adapter_ref[:, columns(h2)])
    own[...] = dot(patches_ref[...], adapter_ref[:, columns(h)])
    half.wait_recv()
    cross_send[...] = (far + half_recv[1].astype(F32)).astype(BF16)
    cross = send(cross_send, cross_recv, 3, h2)
    own[...] = own[...] + half_recv[0].astype(F32)

    text_cross.wait_recv()
    text_relay = send(gath.at[1, h2], gath.at[1, h2], 4, h1)
    text_pair.wait_recv()
    text_relay.wait_recv()

    def project(k):
        blocks = [gath[k, b].astype(F32) for b in range(4)]
        square = sum(jnp.sum(x * x, axis=1, keepdims=True) for x in blocks)
        scale = lax.rsqrt(square / (4 * width) + EPSILON)
        for b in range(4):
            gain = gain_ref[:, b * width : (b + 1) * width]
            normed[:, b * width : (b + 1) * width] = (blocks[b] * scale * gain).astype(BF16)
        for q in range(4):
            proj[k, q] = dot(normed[...], w_in[:, q * width : (q + 1) * width]).astype(BF16)
        preact = dot(normed[...], decay_ref[...])
        decay = -ceiling_ref[...] * jax.nn.sigmoid(preact)
        if k == 0:
            decay = decay + jnp.where(iota(decay.shape, 0) == 0, burst_ref[...], 0.0)
        lower = (iota((rows, rows), 0) >= iota((rows, rows), 1)).astype(F32)
        within = exact_dot(lower, decay)
        within_keep[k] = within
        span_send[k : k + 1, :] = within[rows - 1 :, :]

    def attend(k):
        within = within_keep[k]
        across = within.T
        tail = jnp.exp(within[rows - 1 :, :] - within)
        causal = iota((rows, rows), 0) >= iota((rows, rows), 1)
        for i in range(heads):
            lane = slice(i * LANES, (i + 1) * LANES)
            query, key, value = (proj[k, q, :, lane] for q in range(3))
            scores = lax.dot_general(
                query, key, (((1,), (1,)), ((), ())), preferred_element_type=F32
            )
            lagged = within[:, i : i + 1] - across[i : i + 1, :]
            fade = jnp.exp(jnp.where(causal, lagged, 0.0))
            weights = jnp.where(causal, scores * fade, 0.0).astype(BF16)
            inner[k, :, lane] = dot(weights, value)
            weighted = key.astype(F32) * tail[:, i : i + 1]
            state[k, lane, :] = dot(weighted.T.astype(BF16), value).astype(BF16)

    span_send[...] = jnp.zeros_like(span_send)
    in_load.wait()
    project(1)

    cross.wait_recv()
    gath[0, h] = (own[...] + cross_recv[...].astype(F32)).astype(BF16)
    image_cross = send(gath.at[0, h], gath.at[0, h], 5, h2)
    image_pair = send(gath.at[0, h], gath.at[0, h], 6, h1)
    attend(1)
    image_cross.wait_recv()
    image_relay = send(gath.at[0, h2], gath.at[0, h2], 7, h1)
    image_pair.wait_recv()
    image_relay.wait_recv()
    project(0)

    def spread(source, target, send_sem, recv_sem):
        copies = []
        for j in range(1, n):
            peer = lax.rem(me + j, n)
            copy = pltpu.make_async_remote_copy(
                src_ref=source(peer),
                dst_ref=target,
                send_sem=send_sem.at[j],
                recv_sem=recv_sem.at[j],
                device_id={"seq": peer},
            )
            copy.start()
            copies.append(copy)
        sent.extend(copies)
        return copies

    def piece(device):
        return pl.ds(pl.multiple_of(device * part, part), part)

    spans = spread(lambda peer: span_send, span_recv.at[me], span_send_sem, span_recv_sem)
    span_recv[me] = span_send[...]
    attend(0)
    states = spread(
        lambda peer: state.at[:, piece(peer)], state_recv.at[me], state_send_sem, state_recv_sem
    )
    keep_state = pltpu.make_async_copy(state.at[:, piece(me)], state_recv.at[me], keep_sem.at[0])
    keep_state.start()

    for copy in spans:
        copy.wait_recv()
    units = SPAN_ROWS * n
    my_head = (me * part) // LANES
    table = span_recv[...].reshape(units, LANES)
    span_col = jnp.sum(
        jnp.where(iota(table.shape, 1) == my_head, table, 0.0), axis=1, keepdims=True
    )
    eye = iota((units, units), 0) == iota((units, units), 1)
    span_row = jnp.sum(jnp.where(eye, span_col, 0.0), axis=0, keepdims=True)
    place_row, place_col = place_row_ref[...], place_col_ref[...]
    earlier = place_row < place_col
    later = place_col < place_row
    begin_col = jnp.sum(jnp.where(earlier, span_row, 0.0), axis=1, keepdims=True)
    begin_row = jnp.sum(jnp.where(later, span_col, 0.0), axis=0, keepdims=True)
    passed = jnp.minimum(begin_col - begin_row - span_row, 0.0)
    share = jnp.where(earlier, jnp.exp(passed), 0.0)
    share_high = share.astype(BF16)
    share_low = (share - share_high.astype(F32)).astype(BF16)
    total = 2 * n * part

    def unit_of(index):
        return index // (2 * part) * SPAN_ROWS + (index // part) % 2

    tall = (unit_of(iota((total, units), 0)) == iota((total, units), 1)).astype(BF16)
    wide = (unit_of(iota((units, total), 1)) == iota((units, total), 0)).astype(BF16)
    same = iota((total, total), 0) % part == iota((total, total), 1) % part

    def expand(values):
        grid = dot(dot(tall, values).astype(BF16), wide)
        return jnp.where(same, grid, 0.0).astype(BF16)

    mix_high = expand(share_high)
    mix_low = expand(share_low)
    keep_state.wait()
    for copy in states:
        copy.wait_recv()
    every = state_recv[...].reshape(total, LANES)
    joined = dot(mix_high, every) + dot(mix_low, every)
    entering_send[...] = joined.astype(BF16).reshape(n, 2, part, LANES)
    enters = spread(
        lambda peer: entering_send.at[peer],
        entering.at[:, piece(me)],
        enter_send_sem,
        enter_recv_sem,
    )
    keep_enter = pltpu.make_async_copy(
        entering_send.at[me], entering.at[:, piece(me)], keep_sem.at[1]
    )
    keep_enter.start()
    out_load.wait()
    keep_enter.wait()
    for copy in enters:
        copy.wait_recv()

    def finish(k):
        grown = jnp.exp(within_keep[k])
        pieces = []
        for i in range(heads):
            lane = slice(i * LANES, (i + 1) * LANES)
            carried = grown[:, i : i + 1] * dot(proj[k, 0, :, lane], entering[k, lane, :])
            attended = inner[k, :, lane] + carried
            mean_square = jnp.mean(attended * attended, axis=1, keepdims=True)
            unit = attended * lax.rsqrt(mean_square + EPSILON) * out_gain_ref[i : i + 1, :]
            gate = proj[k, 3, :, lane].astype(F32)
            pieces.append((unit * gate * jax.nn.sigmoid(gate)).astype(BF16))
        gated = jnp.concatenate(pieces, axis=1)
        out_send[k, 0] = dot(gated, w_out[:, columns(h3)]).astype(BF16)
        out_send[k, 1] = dot(gated, w_out[:, columns(h1)]).astype(BF16)
        copy = send(out_send.at[k], out_recv.at[k], 8 + k, h1)
        distant = dot(gated, w_out[:, columns(h2)])
        out_own[k] = dot(gated, w_out[:, columns(h)])
        copy.wait_recv()
        out_cross_send[k] = (distant + out_recv[k, 0].astype(F32)).astype(BF16)
        return send(out_cross_send.at[k], out_cross_recv.at[k], 10 + k, h2)

    def result(k):
        total_out = out_own[k] + out_recv[k, 1].astype(F32) + out_cross_recv[k].astype(F32)
        return (gath[k, h].astype(F32) + total_out).astype(BF16)

    first = finish(0)
    second = finish(1)
    first.wait_recv()
    image_out_ref[0] = result(0)
    second.wait_recv()
    text_out_ref[...] = result(1)
    for copy in sent:
        copy.wait_send()


def shards(
    image_patches,
    text_embed,
    image_start,
    image_forget,
    adapter,
    norm_gain,
    in_proj,
    decay_proj,
    head_decay_ceiling,
    out_gain,
    out_proj,
):
    n = lax.axis_size("seq")
    me = lax.axis_index("seq")
    rows, width = text_embed.shape
    model_width = in_proj.shape[0]
    heads = head_decay_ceiling.shape[0]
    part = heads * LANES // n
    places = unit_places(image_start, n)
    places = jnp.pad(places, ((0, 0), (0, SPAN_ROWS - 2)), constant_values=0).reshape(-1)
    used = jnp.arange(SPAN_ROWS * n) % SPAN_ROWS < 2
    place_row = jnp.where(used, places, 4 * n)[None, :]
    place_col = jnp.where(used, places, 4 * n)[:, None]
    burst = jnp.log1p(-lax.dynamic_index_in_dim(image_forget, me, 0, True))
    burst = jnp.broadcast_to(burst[None, :], (1, LANES))
    decay_pad = jnp.pad(decay_proj, ((0, 0), (0, LANES - heads)))
    ceiling = jnp.pad(head_decay_ceiling, (0, LANES - heads))[None, :]
    vmem = pl.BlockSpec(memory_space=pltpu.VMEM)
    hbm = pl.BlockSpec(memory_space=pl.ANY)
    dma = pltpu.SemaphoreType.DMA
    return pl.pallas_call(
        functools.partial(layer_kernel, n, heads),
        out_shape=(
            jax.ShapeDtypeStruct((1, rows, width), BF16),
            jax.ShapeDtypeStruct((rows, width), BF16),
        ),
        in_specs=[vmem] * 10 + [hbm] * 2,
        out_specs=(vmem, vmem),
        scratch_shapes=[
            pltpu.VMEM((model_width, 4 * width), BF16),
            pltpu.VMEM((width, model_width), BF16),
            pltpu.VMEM((2, 4, rows, width), BF16),
            pltpu.VMEM((rows, model_width), BF16),
            pltpu.VMEM((2, 4, rows, width), BF16),
            pltpu.VMEM((2, rows, width), F32),
            pltpu.VMEM((2, rows, LANES), F32),
            pltpu.VMEM((2, rows, width), BF16),
            pltpu.VMEM((2, rows, width), BF16),
            pltpu.VMEM((rows, width), F32),
            pltpu.VMEM((rows, width), BF16),
            pltpu.VMEM((rows, width), BF16),
            pltpu.VMEM((2, 2, rows, width), BF16),
            pltpu.VMEM((2, 2, rows, width), BF16),
            pltpu.VMEM((2, rows, width), BF16),
            pltpu.VMEM((2, rows, width), BF16),
            pltpu.VMEM((2, rows, width), F32),
            pltpu.VMEM((2, heads * LANES, LANES), BF16),
            pltpu.VMEM((n, 2, part, LANES), BF16),
            pltpu.VMEM((n, 2, part, LANES), BF16),
            pltpu.VMEM((2, heads * LANES, LANES), BF16),
            pltpu.VMEM((SPAN_ROWS, LANES), F32),
            pltpu.VMEM((n, SPAN_ROWS, LANES), F32),
            dma((2,)),
            dma((12,)),
            dma((12,)),
            dma((n,)),
            dma((n,)),
            dma((n,)),
            dma((n,)),
            dma((n,)),
            dma((n,)),
            dma((2,)),
        ],
        compiler_params=pltpu.CompilerParams(
            collective_id=0, has_side_effects=True, vmem_limit_bytes=60 * 1024 * 1024
        ),
    )(
        image_patches[0],
        text_embed,
        adapter,
        norm_gain[None, :],
        decay_pad,
        ceiling,
        burst,
        out_gain,
        place_row,
        place_col,
        in_proj.reshape(model_width, -1),
        out_proj,
    )


def solution(mesh):
    in_specs = (
        P("seq", None, "head"),
        P("seq", "head"),
        P(),
        P(),
        P("head", None),
        P(),
        P(None, None, "head"),
        P(None, "head"),
        P("head"),
        P("head", None),
        P("head", None),
    )
    out_specs = (P("seq", None, "head"), P("seq", "head"))
    return jax.shard_map(shards, mesh=mesh, in_specs=in_specs, out_specs=out_specs, check_vma=False)
```

time: 191 us -> 92 us (0.48)
  waiting for transfers between devices: 94.6 us -> 0 us
  Pallas kernels: 0 us -> 66.7 us
  matrix products: 24.1 us -> 0 us
  blocking collectives: 20.7 us -> 0 us
  between operations: 14.7 us -> 1.35 us
  other arithmetic: 11.1 us -> 2.89 us
  local copies, waits for them, and re-layouts: 24.9 us -> 20.6 us
    pallas_call x0 -> x1, Pallas kernels: none -> 66.7 us  [shards(): pl.pallas_call(functools.partial(layer_kernel, n, heads), out_shape=(jax....]
    reduce_scatter x2 -> x0, waiting for transfers between devices: 57.5 us -> none  [the longest x1 29.9 us: shards(): lax.psum_scatter(partial_out.astype(jnp.bfloat16), 'head', scatter_dimens...]
    all_gather x2 -> x0, waiting for transfers between devices: 37.1 us -> none  [the longest x1 26 us: shards(): all_state = lax.all_gather(state.astype(jnp.bfloat16), 'seq')]
    dot_general x7 -> x0, matrix products: 24.1 us -> none  [the longest x1 9.97 us: shards(): jnp.dot(normed, in_proj.reshape(model_width, -1), preferred_element_type=...]
    all_gather x1 -> x0, blocking collectives: 20.7 us -> none  [shards(): all_span = lax.all_gather(span, 'seq')]
    convert_element_type x3 -> x0, other arithmetic: 4.87 us -> none  [the longest x1 2.1 us: shards(): all_state.reshape(1, 2 * seq_count, heads, head_width, head_width)]
    slice x6 -> x0, local copies, waits for them, and re-layouts: 4.47 us -> none  [the longest x1 3.21 us: shards(): queries, keys, values, gates = (projected[:, :, i] for i in range(4))]
    reshape x4 -> x2, local copies, waits for them, and re-layouts: 4.48 us -> 0.15 us  [shards(): jnp.pad(places, ((0, 0), (0, SPAN_ROWS - 2)), constant_values=0).reshape(-1)]
  transfers between devices with their start and end apart: 4 -> 0, of which waited for: 4 -> 0; matrix products, arithmetic and copies ran while one was open for 7% -> 0% of each run, Pallas kernels for 0% -> 0%
where the time goes in v2:
time: 92 us; the launch traced here: 91.5 us
  Pallas kernels  66.7 us (72%)
  local copies, waits for them, and re-layouts  20.6 us (22%)
  other arithmetic  2.89 us (3%)
  between operations  1.35 us (1%)
    pallas_call x1, Pallas kernels, shards(): pl.pallas_call(functools.partial(layer_kernel, n, heads), out_shape=(jax....  66.7 us
    unnamed x6, local copies, waits for them, and re-layouts  16.4 us

profile of v2, /device:TPU:0, one launch (start us, length us, event | category | flops | bytes accessed | tf_op | source)
XLA Modules:
  0.0 91.5 jit_solution(14658214610859303585)
XLA Ops:
  0.6 1.2 %dynamic_slice.4 = f32[1]{0:T(128)} dynamic-slice(f32[8]{0:T(128)} %param.14, s32[]{:T(128)S(6)} %select_n.53), dynamic_slice_sizes={1} | dynamic-slice | bytes 12 | tf_op jit(solution)/shard_map/jit(dynamic_index_in_dim)/dynamic_slice | solution.py:342
  2.6 0.6 broadcast_in_dim.18.burst_ref
  3.2 1.2 %pad_bitcast_fusion.ceiling_ref = f32[1,128]{1,0:T(1,128)} fusion(f32[4]{0:T(128)} %param.19), kind=kLoop, calls=%fused_computation.21 | loop fusion | bytes 528 | tf_op jit(solution)/shard_map/broadcast_in_dim | solution.py:345
  4.4 0.7 fusion.6
  5.0 0.7 and_select_fusion
  5.7 0.1 convert_reduce_fusion
  5.8 0.1 select_reduce_fusion
  5.9 0.1 select_reduce_fusion.1
  6.0 0.1 copy.23
  6.1 0.1 reshape.94
  6.2 0.6 compare_select_fusion.place_row_ref
  6.8 0.1 reshape.97
  6.9 0.6 fusion.4.place_col_ref
  7.5 1.7 %copy.18 = bf16[1,256,288]{2,1,0:T(8,128)(2,1)} copy(bf16[1,256,288]{1,2,0:T(8,128)(2,1)} %param.11) | data formatting | bytes 294912 | tf_op args[0]
  9.2 1.0 %copy.19 = bf16[2048,4]{1,0:T(8,128)(2,1)S(1)} copy(bf16[2048,4]{0,1:T(4,128)(2,1)} %param.18) | data formatting | bytes 32768 | tf_op args[7]
  10.3 1.0 %pad.12.decay_ref = bf16[2048,128]{1,0:T(8,128)(2,1)} pad(bf16[2048,4]{1,0:T(8,128)(2,1)S(1)} %copy.19, bf16[]{:T(256)} %constant.44.clone.1), padding=0_0x0_124 | pad | bytes 540674 | tf_op jit(solution)/shard_map/jit(_pad)/pad | solution.py:344
  11.2 10.2 %copy.24 = bf16[256,8,4,512]{3,1,2,0:T(8,128)(2,1)} copy(bf16[256,8,4,512]{3,2,1,0:T(4,128)(2,1)} %bitcast.11) | data formatting | bytes 16777216
  21.5 66.7 %shard_map.122 = (bf16[1,256,512]{2,1,0:T(8,128)(2,1)}, bf16[256,512]{1,0:T(8,128)(2,1)}) custom-call(bf16[256,288]{1,0:T(8,128)(2,1)} %bitcast.12, bf16[256,512]{1,0:T(8,128)(2,1)} %text_ref.1, bf16[288,2048]{1,0:T(8,128)(2,1)} %adapter_ref.1, f32[1,2048]{1,0:T(1,128)} %bitcast.13, bf16[2048,128]{1,0:T(8,128)(2,1)} %pad.12.decay_ref, ...), custom_call_target="tpu_custom_call" | custom-call | tf_op jit(solution)/shard_map/pallas_call | solution.py:349
  88.2 1.7 %copy.27 = bf16[1,256,512]{2,1,0:T(8,128)(2,1)} copy(bf16[1,256,512]{2,1,0:T(8,128)(2,1)} %get-tuple-element.4) | data formatting | bytes 524288
  89.8 1.7 %copy.28 = bf16[256,512]{1,0:T(8,128)(2,1)} copy(bf16[256,512]{1,0:T(8,128)(2,1)} %get-tuple-element.5) | data formatting | bytes 524288
  (4 shorter events, 0.0 us)

commit v3 on v2

--- a/solution.py
+++ b/solution.py
@@ -57,6 +57,8 @@
     out_proj_ref,
     image_out_ref,
     text_out_ref,
+    w_raw,
+    w_flat,
     w_in,
     w_out,
     gath,
@@ -98,7 +100,7 @@
     h3 = lax.rem(h1 + 2, 4)
     rows, width = text_ref.shape
     part = heads * LANES // n
-    in_load = pltpu.make_async_copy(in_proj_ref, w_in, load_sem.at[0])
+    in_load = pltpu.make_async_copy(in_proj_ref.reshape(4 * in_proj_ref.shape[0], width), w_raw, load_sem.at[0])
     out_load = pltpu.make_async_copy(out_proj_ref, w_out, load_sem.at[1])
     in_load.start()
     out_load.start()
@@ -141,6 +143,26 @@
     cross = send(cross_send, cross_recv, 3, h2)
     own[...] = own[...] + half_recv[0].astype(F32)
 
+    in_load.wait()
+    step_rows = 128
+
+    @pl.loop(0, w_in.shape[1] // step_rows)
+    def _(step):
+        flat = w_raw[pl.ds(pl.multiple_of(step * 512, 512), 512), :].astype(F32)
+        for b in range(width // LANES):
+            w_flat[b] = flat[:, b * LANES : (b + 1) * LANES]
+        for q in range(4):
+            for c in range(step_rows // 64):
+                taken = jnp.concatenate(
+                    [
+                        w_flat[b, pl.ds(c * 256 + q, 64, stride=4), :]
+                        for b in range(width // LANES)
+                    ],
+                    axis=1,
+                )
+                base = pl.multiple_of(step * step_rows + c * 64, 64)
+                w_in[q, pl.ds(base, 64), :] = taken.astype(BF16)
+
     text_cross.wait_recv()
     text_relay = send(gath.at[1, h2], gath.at[1, h2], 4, h1)
     text_pair.wait_recv()
@@ -154,7 +176,7 @@
             gain = gain_ref[:, b * width : (b + 1) * width]
             normed[:, b * width : (b + 1) * width] = (blocks[b] * scale * gain).astype(BF16)
         for q in range(4):
-            proj[k, q] = dot(normed[...], w_in[:, q * width : (q + 1) * width]).astype(BF16)
+            proj[k, q] = dot(normed[...], w_in[q]).astype(BF16)
         preact = dot(normed[...], decay_ref[...])
         decay = -ceiling_ref[...] * jax.nn.sigmoid(preact)
         if k == 0:
@@ -183,7 +205,6 @@
             state[k, lane, :] = dot(weighted.T.astype(BF16), value).astype(BF16)
 
     span_send[...] = jnp.zeros_like(span_send)
-    in_load.wait()
     project(1)
 
     cross.wait_recv()
@@ -355,7 +376,9 @@
         in_specs=[vmem] * 10 + [hbm] * 2,
         out_specs=(vmem, vmem),
         scratch_shapes=[
-            pltpu.VMEM((model_width, 4 * width), BF16),
+            pltpu.VMEM((4 * model_width, width), BF16),
+            pltpu.VMEM((width // LANES, 512, LANES), F32),
+            pltpu.VMEM((4, model_width, width), BF16),
             pltpu.VMEM((width, model_width), BF16),
             pltpu.VMEM((2, 4, rows, width), BF16),
             pltpu.VMEM((rows, model_width), BF16),
@@ -403,7 +426,7 @@
         out_gain,
         place_row,
         place_col,
-        in_proj.reshape(model_width, -1),
+        in_proj,
         out_proj,
     )
 

time: 92 us -> 81.5 us (0.89)
  local copies, waits for them, and re-layouts: 20.6 us -> 10.2 us
    unnamed x6 -> x5, local copies, waits for them, and re-layouts: 16.4 us -> 6.17 us
where the time goes in v3:
time: 81.5 us; the launch traced here: 81.1 us
  Pallas kernels  66.6 us (82%)
  local copies, waits for them, and re-layouts  10.2 us (13%)
  other arithmetic  2.85 us (3%)
  between operations  1.35 us (2%)
    pallas_call x1, Pallas kernels, shards(): pl.pallas_call(functools.partial(layer_kernel, n, heads), out_shape=(jax....  66.6 us
    unnamed x5, local copies, waits for them, and re-layouts  6.17 us

profile of v3, /device:TPU:0, one launch (start us, length us, event | category | flops | bytes accessed | tf_op | source)
XLA Modules:
  0.0 81.1 jit_solution(12471146777764850185)
XLA Ops:
  0.6 1.2 %dynamic_slice.4 = f32[1]{0:T(128)} dynamic-slice(f32[8]{0:T(128)} %param.14, s32[]{:T(128)S(6)} %select_n.53), dynamic_slice_sizes={1} | dynamic-slice | bytes 12 | tf_op jit(solution)/shard_map/jit(dynamic_index_in_dim)/dynamic_slice | solution.py:363
  2.6 0.5 broadcast_in_dim.18.burst_ref
  3.1 1.2 %pad_bitcast_fusion.ceiling_ref = f32[1,128]{1,0:T(1,128)} fusion(f32[4]{0:T(128)} %param.19), kind=kLoop, calls=%fused_computation.21 | loop fusion | bytes 528 | tf_op jit(solution)/shard_map/broadcast_in_dim | solution.py:366
  4.3 0.7 fusion.6
  5.0 0.7 and_select_fusion
  5.7 0.1 convert_reduce_fusion
  5.8 0.1 select_reduce_fusion
  5.9 0.1 select_reduce_fusion.1
  6.0 0.1 copy.23
  6.1 0.1 reshape.91
  6.2 0.6 compare_select_fusion.place_row_ref
  6.7 0.1 reshape.93
  6.8 0.6 fusion.4.place_col_ref
  7.4 1.7 %copy.18 = bf16[1,256,288]{2,1,0:T(8,128)(2,1)} copy(bf16[1,256,288]{1,2,0:T(8,128)(2,1)} %param.11) | data formatting | bytes 294912 | tf_op args[0]
  9.2 1.0 %copy.19 = bf16[2048,4]{1,0:T(8,128)(2,1)S(1)} copy(bf16[2048,4]{0,1:T(4,128)(2,1)} %param.18) | data formatting | bytes 32768 | tf_op args[7]
  10.2 0.9 %pad.12.decay_ref = bf16[2048,128]{1,0:T(8,128)(2,1)} pad(bf16[2048,4]{1,0:T(8,128)(2,1)S(1)} %copy.19, bf16[]{:T(256)} %constant.44.clone.1), padding=0_0x0_124 | pad | bytes 540674 | tf_op jit(solution)/shard_map/jit(_pad)/pad | solution.py:365
  11.1 66.6 %shard_map.122 = (bf16[1,256,512]{2,1,0:T(8,128)(2,1)}, bf16[256,512]{1,0:T(8,128)(2,1)}) custom-call(bf16[256,288]{1,0:T(8,128)(2,1)} %bitcast.8, bf16[256,512]{1,0:T(8,128)(2,1)} %text_ref.1, bf16[288,2048]{1,0:T(8,128)(2,1)} %adapter_ref.1, f32[1,2048]{1,0:T(1,128)} %bitcast.9, bf16[2048,128]{1,0:T(8,128)(2,1)} %pad.12.decay_ref, ...), custom_call_target="tpu_custom_call" | custom-call | tf_op jit(solution)/shard_map/pallas_call | solution.py:370
  77.7 1.7 %copy.26 = bf16[1,256,512]{2,1,0:T(8,128)(2,1)} copy(bf16[1,256,512]{2,1,0:T(8,128)(2,1)} %get-tuple-element.4) | data formatting | bytes 524288
  79.4 1.7 %copy.27 = bf16[256,512]{1,0:T(8,128)(2,1)} copy(bf16[256,512]{1,0:T(8,128)(2,1)} %get-tuple-element.5) | data formatting | bytes 524288
  (4 shorter events, 0.0 us)
